TPU v7x, 256 devices: a whole 4x4x8 slice. The times are simulated.
256 devices in a mesh: dp: 128 (over y, z, x), mp: 2 (over core).
Axes of the slice: x: 4, y: 4, z: 8, core: 2. Of those that a mesh axis runs over, the one named last changes fastest.
Arguments:
- grad: bfloat16 [32, 1024, 8192], P(None, 'dp', 'mp'), may hold values from -6 to 6
- second_moment: float32 [32, 1024, 8192], P(None, 'dp', 'mp'), may hold values from 0.004 to 20, as said below
- left_root: bfloat16 [2, 128, 1024, 1024], P('mp', 'dp'), as said below
- right_root: bfloat16 [2, 128, 1024, 1024], P('mp', 'dp'), as said below
- owner_slot: int32 [2, 32, 4], replicated, may hold values from 0 to 127, as said below
Outputs:
- update: bfloat16 [32, 1024, 8192], P(None, 'dp', 'mp')
Inputs may be any that keep to these rules, and one draw needn't show every extreme that they name: For each h, owner_slot[h] lists every dp index exactly once: each dp index owns one block of each h. `second_moment`: positive. `left_root`: each square is symmetric positive definite. `right_root`: each square is symmetric positive definite.
All inputs are finite; a program needn't handle non-finite values.
Results may differ from a plain program's by a relative error of at most 0.0049.
Values may be sent and summed in bfloat16 or wider, within the bound.
No kernel may reach another device: no remote copies, remote signals or barrier semaphores. Data moves between devices by JAX's collectives and lax.ppermute only.
A program may use at most 64 MiB of HBM per device.

v0:
```python
import jax
import jax.numpy as jnp
from jax import lax
from jax.sharding import Mesh
from jax.sharding import PartitionSpec as P

DP = ("dp_0", "dp_1", "dp_2")
BETA_TWO = 0.99
ADAM_EPS = 1e-08
NORM_EPS = 1e-06


def one_axis_at_a_time(value, axes):
    for axis in axes:
        value = lax.psum(value, axis)
    return value


def per_device(grad, second_moment, left_root, right_root, owner_slot):
    row_blocks, block_rows, half_cols = grad.shape
    block_size = left_root.shape[-1]
    col_blocks = half_cols // block_size
    dp_count = lax.axis_size(DP)
    mp_index = lax.axis_index("mp")
    owner_index = lax.axis_index(DP)
    widened = grad.astype(jnp.float32)
    moment_new = BETA_TWO * second_moment + (1.0 - BETA_TWO) * widened * widened
    direction = widened / (jnp.sqrt(moment_new) + ADAM_EPS)
    partial_value = jnp.sum(
        (direction * direction).reshape(row_blocks, block_rows, col_blocks, block_size), axis=(1, 3)
    )
    table = lax.dynamic_index_in_dim(owner_slot, mp_index, 0, keepdims=False)
    owner_ids = lax.iota(jnp.int32, dp_count)
    matches = table[None, :, :] == owner_ids[:, None, None]
    select_half = matches.astype(jnp.bfloat16)
    select_full = matches.astype(jnp.float32).reshape(dp_count, row_blocks * col_blocks)
    tiles = grad.reshape(row_blocks, block_rows, col_blocks, block_size)
    outgoing = jnp.einsum("src,rwck->swk", select_half, tiles, preferred_element_type=jnp.float32)
    outgoing = outgoing.astype(jnp.bfloat16).reshape(dp_count, 1, block_rows, block_size)
    totals = one_axis_at_a_time(partial_value, DP)
    own_row = lax.dynamic_index_in_dim(select_full, owner_index, 0, keepdims=False)
    adam_sq = jnp.sum(own_row * totals.reshape(-1))
    left = left_root[0, 0]
    right = right_root[0, 0]
    rows_in = lax.all_to_all(outgoing, DP, split_axis=0, concat_axis=1, tiled=True)
    flat = rows_in.reshape(-1, block_size)
    product = jnp.dot(flat, right, preferred_element_type=jnp.float32).astype(jnp.bfloat16)
    mixed_rows = product.reshape(rows_in.shape)
    mixed = mixed_rows.reshape(block_size, block_size)
    shaped = jnp.dot(left, mixed, preferred_element_type=jnp.float32)
    shaped_sq = jnp.sum(shaped * shaped)
    factor = jnp.sqrt((adam_sq + NORM_EPS) / (shaped_sq + NORM_EPS))
    result = (shaped * factor).astype(jnp.bfloat16).reshape(1, dp_count, block_rows, block_size)
    back = lax.all_to_all(result, DP, split_axis=1, concat_axis=0, tiled=True)
    placed = jnp.einsum(
        "src,swk->rwck",
        select_half,
        back.reshape(dp_count, block_rows, block_size),
        preferred_element_type=jnp.float32,
    )
    return placed.astype(jnp.bfloat16).reshape(row_blocks, block_rows, half_cols)


def solution(mesh):
    split = Mesh(mesh.devices.reshape(4, 8, 4, mesh.shape["mp"]), ("dp_0", "dp_1", "dp_2", "mp"))
    return jax.shard_map(
        per_device,
        mesh=split,
        in_specs=(
            P(None, DP, "mp"),
            P(None, DP, "mp"),
            P("mp", DP, None, None),
            P("mp", DP, None, None),
            P(),
        ),
        out_specs=P(None, DP, "mp"),
        check_vma=False,
    )
```

profile of v0, /device:TPU:32, one launch (start us, length us, event | category | flops | bytes accessed | tf_op | source)
XLA Modules:
  0.0 170.4 jit_solution(4554805656612453106)
XLA Ops:
  0.0 0.0 copy-start
  0.0 0.8 fusion.41
  0.8 4.4 %fusion.18 = bf16[128,1,8,1024]{3,0,2,1:T(8,128)(2,1)S(1)} fusion(bf16[32,8,4,1024]{3,1,2,0:T(8,128)(2,1)} %bitcast.59, s32[32,4]{0,1:T(4,128)S(1)} %fusion.41), kind=kOutput, calls=%fused_computation.22 | convolution fusion | flops 269500416 | bytes 4194816 | tf_op jit(solution)/shard_map/src,rwck->swk/dot_general | solution.py:38
  5.2 2.5 %copy.28 = bf16[128,1,8,1024]{3,2,1,0:T(8,128)(2,1)} copy(bf16[128,1,8,1024]{3,0,2,1:T(8,128)(2,1)S(1)} %fusion.18) | data formatting | bytes 4194304 | tf_op jit(solution)/shard_map/reshape | solution.py:39
  7.7 0.0 copy-start.1
  7.7 15.6 %all-to-all-start = ((bf16[128,1,8,1024]{3,2,1,0:T(8,128)(2,1)}), bf16[128,1,8,1024]{3,2,1,0:T(8,128)(2,1)}, u32[]{:S(2)}, u32[]{:S(2)}) async-start(bf16[128,1,8,1024]{3,2,1,0:T(8,128)(2,1)} %copy.28), calls=%async_computation | async-start | bytes 4194304 | tf_op jit(solution)/shard_map/all_to_all | solution.py:45
  23.3 0.0 copy-done.1
  23.3 0.1 copy.29
  23.4 0.1 eq.28
  23.5 6.0 %fusion.4 = f32[32,4096]{1,0:T(8,128)S(1)} fusion(f32[32,8,4096]{2,1,0:T(8,128)} %param.6, bf16[32,8,4096]{2,1,0:T(8,128)(2,1)} %param.5), kind=kLoop, calls=%fused_computation.9 | loop fusion | flops 9306112 | bytes 6815744 | tf_op jit(solution)/shard_map/reduce_sum | solution.py:29
  29.5 0.4 reduce_sum.35
  29.9 0.1 reduce_sum.36
  30.0 0.1 copy.37
  30.1 11.2 %psum.21 = f32[32,4]{0,1:T(4,128)S(1)} all-reduce(f32[32,4]{0,1:T(4,128)S(1)} %copy.37), channel_id=1, replica_groups=mesh['dp_0'=4,'dp_1'=8,'dp_2'=4,'mp'=2] {'dp_0'}, use_global_device_ids=true, to_apply=%region_2.3 | all-reduce | flops 128 | bytes 1024 | tf_op jit(solution)/shard_map/psum | solution.py:15
  41.3 36.2 %psum.22 = f32[32,4]{0,1:T(4,128)S(1)} all-reduce(f32[32,4]{0,1:T(4,128)S(1)} %psum.21), channel_id=1, replica_groups=mesh['dp_0'=4,'dp_1'=8,'dp_2'=4,'mp'=2] {'dp_1'}, use_global_device_ids=true, to_apply=%region_3.4 | all-reduce | flops 128 | bytes 1024 | tf_op jit(solution)/shard_map/psum | solution.py:15
  77.5 0.1 copy.31
  77.6 0.1 reshape.37
  77.7 10.8 %psum.23 = f32[128]{0:T(128)S(1)} all-reduce(f32[128]{0:T(128)S(1)} %reshape.37), channel_id=1, replica_groups=mesh['dp_0'=4,'dp_1'=8,'dp_2'=4,'mp'=2] {'dp_2'}, use_global_device_ids=true, to_apply=%region_4.5 | all-reduce | flops 128 | bytes 1024 | tf_op jit(solution)/shard_map/psum | solution.py:15
  88.5 0.7 fusion.36
  89.9 0.0 all-to-all-done
  89.9 0.0 copy-done
  89.9 9.2 %multiply_reduce_fusion = (f32[]{:T(128)}, f32[1024,1024]{0,1:T(8,128)}) fusion(bf16[1,1,1024,1024]{3,2,1,0:T(8,128)(2,1)S(1)} %copy-done, bf16[128,1,8,1024]{3,2,1,0:T(8,128)(2,1)} %all-to-all-done, bf16[1,1,1024,1024]{3,2,1,0:T(8,128)(2,1)} %param.7), kind=kOutput, calls=%fused_computation.8 | convolution fusion | flops 4298113024 | bytes 10485764 | tf_op jit(solution)/shard_map/dot_general | solution.py:50
  99.9 2.8 %fusion.5 = bf16[1,128,8,1024]{3,2,0,1:T(8,128)(2,1)S(1)} fusion(f32[1024,1024]{0,1:T(8,128)} %get-tuple-element.6, f32[]{:T(128)S(6)} %sqrt.7), kind=kLoop, calls=%fused_computation.10 | loop fusion | flops 2097152 | bytes 6291460 | tf_op jit(solution)/shard_map/reshape | solution.py:53
  102.6 58.6 %all_to_all.8 = bf16[1,128,8,1024]{3,2,0,1:T(8,128)(2,1)S(1)} all-to-all(bf16[1,128,8,1024]{3,2,0,1:T(8,128)(2,1)S(1)} %fusion.5), channel_id=1, replica_groups=mesh['dp_0'=4,'dp_1'=8,'dp_2'=4,'mp'=2] {'dp_0','dp_1','dp_2'}, dimensions={1} | all-to-all | bytes 4194304 | tf_op jit(solution)/shard_map/all_to_all | solution.py:54
  161.2 1.7 %convert_bitcast_fusion = bf16[32,8,4,1024]{3,0,2,1:T(8,128)(2,1)S(1)} fusion(bf16[1,128,8,1024]{3,2,0,1:T(8,128)(2,1)S(1)} %all_to_all.8, s32[32,4]{0,1:T(4,128)S(1)} %fusion.41), kind=kOutput, calls=%fused_computation.20 | convolution fusion | flops 269500416 | bytes 4194816 | tf_op jit(solution)/shard_map/src,swk->rwck/dot_general | solution.py:55
  163.0 3.0 %copy.34 = bf16[32,8,4,1024]{3,2,1,0:T(4,128)(2,1)} copy(bf16[32,8,4,1024]{3,0,2,1:T(8,128)(2,1)S(1)} %convert_bitcast_fusion) | data formatting | bytes 4194304 | tf_op jit(solution)/shard_map/convert_element_type | solution.py:61
  165.9 4.5 %reshape.40 = bf16[32,8,4096]{2,1,0:T(8,128)(2,1)} reshape(bf16[32,8,4,1024]{3,2,1,0:T(4,128)(2,1)} %copy.34) | data formatting | bytes 4194304 | tf_op jit(solution)/shard_map/reshape | solution.py:61
  (1 shorter events, 0.0 us)
Async XLA Ops:
  0.0 89.9 %copy-start = (bf16[1,1,1024,1024]{3,2,1,0:T(8,128)(2,1)S(1)}, bf16[1,1,1024,1024]{3,2,1,0:T(8,128)(2,1)}, u32[]{:S(2)}) copy-start(bf16[1,1,1024,1024]{3,2,1,0:T(8,128)(2,1)} %param.8) | copy-start | bytes 6291460
  7.7 15.6 %copy-start.1 = (s32[2,32,4]{1,2,0:T(4,128)S(1)}, s32[2,32,4]{1,2,0:T(4,128)}, u32[]{:S(2)}) copy-start(s32[2,32,4]{1,2,0:T(4,128)} %param.9) | copy-start | bytes 3076
  7.7 82.2 %all-to-all-start = ((bf16[128,1,8,1024]{3,2,1,0:T(8,128)(2,1)}), bf16[128,1,8,1024]{3,2,1,0:T(8,128)(2,1)}, u32[]{:S(2)}, u32[]{:S(2)}) async-start(bf16[128,1,8,1024]{3,2,1,0:T(8,128)(2,1)} %copy.28), calls=%async_computation | async-start | bytes 4194304 | tf_op jit(solution)/shard_map/all_to_all | solution.py:45
where the time goes:
time: 171 us; the launch traced here: 170 us
  blocking collectives  117 us (68%)
  starting transfers between devices  15.6 us (9%)
  matrix products  15.3 us (9%)
  local copies, waits for them, and re-layouts  11.6 us (7%)
  other arithmetic  9.62 us (6%)
    all_to_all x1, blocking collectives, per_device(): back = lax.all_to_all(result, DP, split_axis=1, concat_axis=0, tiled=True)  58.6 us
    psum x3, blocking collectives, one_axis_at_a_time(): value = lax.psum(value, axis)  58.2 us
    all_to_all x1, starting transfers between devices, per_device(): lax.all_to_all(outgoing, DP, split_axis=0, concat_axis=1, tiled=True)  15.6 us
    dot_general x1, matrix products, per_device(): shaped = jnp.dot(left, mixed, preferred_element_type=jnp.float32)  9.24 us
    reduce_sum x2, other arithmetic, per_device(): jnp.sum((direction * direction).reshape(row_blocks, block_rows, col_block...  6.16 us
    reshape x1, local copies, waits for them, and re-layouts, per_device(): placed.astype(jnp.bfloat16).reshape(row_blocks, block_rows, half_cols)  4.45 us
    dot_general x1, matrix products, per_device(): jnp.einsum('src,rwck->swk', select_half, tiles, preferred_element_type=jn...  4.35 us
  transfers between devices with their start and end apart: 1, of which 0 were waited for; matrix products, arithmetic and copies ran while one was open for 5% of the time, Pallas kernels for 0%

commit v1 on v0

--- a/solution.py
+++ b/solution.py
@@ -8,6 +8,14 @@
 BETA_TWO = 0.99
 ADAM_EPS = 1e-08
 NORM_EPS = 1e-06
+
+
+def link_notes(values, comm_axis, in_dim, along_dim):
+    view_out = jax.lax.axis_size(comm_axis)
+    y = jnp.split(values, view_out, in_dim)
+    mixed_arr = jnp.stack(y, 0)
+    r_now = jax.lax.all_to_all(mixed_arr, comm_axis, 0, 0)
+    return jnp.concatenate(r_now, along_dim)
 
 
 def one_axis_at_a_time(value, axes):
@@ -51,7 +59,7 @@
     shaped_sq = jnp.sum(shaped * shaped)
     factor = jnp.sqrt((adam_sq + NORM_EPS) / (shaped_sq + NORM_EPS))
     result = (shaped * factor).astype(jnp.bfloat16).reshape(1, dp_count, block_rows, block_size)
-    back = lax.all_to_all(result, DP, split_axis=1, concat_axis=0, tiled=True)
+    back = link_notes(result, DP, 1, 0)
     placed = jnp.einsum(
         "src,swk->rwck",
         select_half,

time: 171 us -> 182 us (1.064)
  blocking collectives: 117 us -> 126 us
    psum x3, blocking collectives: 58.2 us -> 70.8 us  [one_axis_at_a_time(): value = lax.psum(value, axis)]
    all_to_all x1, blocking collectives: 58.6 us -> 55.4 us  [link_notes(): r_now = jax.lax.all_to_all(mixed_arr, comm_axis, 0, 0)]
  transfers between devices with their start and end apart: 1 -> 1, of which waited for: 0 -> 0; matrix products, arithmetic and copies ran while one was open for 5% -> 4% of each run, Pallas kernels for 0% -> 0%
where the time goes in v1:
time: 182 us; the launch traced here: 181 us
  blocking collectives  126 us (69%)
  starting transfers between devices  15.6 us (9%)
  matrix products  15.3 us (8%)
  local copies, waits for them, and re-layouts  11.9 us (7%)
  other arithmetic  9.62 us (5%)
  between operations  2.54 us (1%)
    psum x3, blocking collectives, one_axis_at_a_time(): value = lax.psum(value, axis)  70.8 us
    all_to_all x1, blocking collectives, link_notes(): r_now = jax.lax.all_to_all(mixed_arr, comm_axis, 0, 0)  55.4 us
    all_to_all x1, starting transfers between devices, per_device(): lax.all_to_all(outgoing, DP, split_axis=0, concat_axis=1, tiled=True)  15.6 us
    dot_general x1, matrix products, per_device(): shaped = jnp.dot(left, mixed, preferred_element_type=jnp.float32)  9.24 us
    reduce_sum x2, other arithmetic, per_device(): jnp.sum((direction * direction).reshape(row_blocks, block_rows, col_block...  6.16 us
    reshape x1, local copies, waits for them, and re-layouts, per_device(): placed.astype(jnp.bfloat16).reshape(row_blocks, block_rows, half_cols)  4.45 us
    dot_general x1, matrix products, per_device(): jnp.einsum('src,rwck->swk', select_half, tiles, preferred_element_type=jn...  4.35 us
  transfers between devices with their start and end apart: 1, of which 0 were waited for; matrix products, arithmetic and copies ran while one was open for 4% of the time, Pallas kernels for 0%

profile of v1, /device:TPU:32, one launch (start us, length us, event | category | flops | bytes accessed | tf_op | source)
XLA Modules:
  0.0 181.1 jit_solution(12323805415066190828)
XLA Ops:
  0.0 0.0 copy-start
  0.0 0.8 fusion.41
  0.8 4.4 %fusion.18 = bf16[128,1,8,1024]{3,0,2,1:T(8,128)(2,1)S(1)} fusion(bf16[32,8,4,1024]{3,1,2,0:T(8,128)(2,1)} %bitcast.570, s32[32,4]{0,1:T(4,128)S(1)} %fusion.41), kind=kOutput, calls=%fused_computation.22 | convolution fusion | flops 269500416 | bytes 4194816 | tf_op jit(solution)/shard_map/src,rwck->swk/dot_general | solution.py:46
  5.2 2.5 %copy.4071 = bf16[128,1,8,1024]{3,2,1,0:T(8,128)(2,1)} copy(bf16[128,1,8,1024]{3,0,2,1:T(8,128)(2,1)S(1)} %fusion.18) | data formatting | bytes 4194304 | tf_op jit(solution)/shard_map/reshape | solution.py:47
  7.7 0.0 copy-start.1
  7.7 15.6 %all-to-all-start = ((bf16[128,1,8,1024]{3,2,1,0:T(8,128)(2,1)}), bf16[128,1,8,1024]{3,2,1,0:T(8,128)(2,1)}, u32[]{:S(2)}, u32[]{:S(2)}) async-start(bf16[128,1,8,1024]{3,2,1,0:T(8,128)(2,1)} %copy.4071), calls=%async_computation | async-start | bytes 4194304 | tf_op jit(solution)/shard_map/all_to_all | solution.py:53
  23.3 0.0 copy-done.1
  23.3 0.1 copy.4072
  23.4 0.1 eq.28
  23.5 6.0 %fusion.4 = f32[32,4096]{1,0:T(8,128)S(1)} fusion(f32[32,8,4096]{2,1,0:T(8,128)} %param.6, bf16[32,8,4096]{2,1,0:T(8,128)(2,1)} %param.5), kind=kLoop, calls=%fused_computation.9 | loop fusion | flops 9306112 | bytes 6815744 | tf_op jit(solution)/shard_map/reduce_sum | solution.py:37
  29.5 0.4 reduce_sum.35
  29.9 0.1 reduce_sum.36
  30.0 17.6 %psum.21 = f32[32,4]{1,0:T(8,128)S(1)} all-reduce(f32[32,4]{1,0:T(8,128)S(1)} %reduce_sum.36), channel_id=1, replica_groups=mesh['dp_0'=4,'dp_1'=8,'dp_2'=4,'mp'=2] {'dp_0'}, use_global_device_ids=true, to_apply=%region_2.3 | all-reduce | flops 128 | bytes 1024 | tf_op jit(solution)/shard_map/psum | solution.py:23
  47.7 42.6 %psum.22 = f32[32,4]{1,0:T(8,128)S(1)} all-reduce(f32[32,4]{1,0:T(8,128)S(1)} %psum.21), channel_id=1, replica_groups=mesh['dp_0'=4,'dp_1'=8,'dp_2'=4,'mp'=2] {'dp_1'}, use_global_device_ids=true, to_apply=%region_3.4 | all-reduce | flops 128 | bytes 1024 | tf_op jit(solution)/shard_map/psum | solution.py:23
  90.2 0.1 reshape.30
  90.3 10.6 %psum.23 = f32[128]{0:T(128)S(1)} all-reduce(f32[128]{0:T(128)S(1)} %reshape.30), channel_id=1, replica_groups=mesh['dp_0'=4,'dp_1'=8,'dp_2'=4,'mp'=2] {'dp_2'}, use_global_device_ids=true, to_apply=%region_4.5 | all-reduce | flops 128 | bytes 1024 | tf_op jit(solution)/shard_map/psum | solution.py:23
  100.9 0.7 fusion.36
  102.3 0.0 all-to-all-done
  102.3 0.0 copy-done
  102.3 9.2 %multiply_reduce_fusion = (f32[]{:T(128)}, f32[1024,1024]{0,1:T(8,128)}) fusion(bf16[1,1,1024,1024]{3,2,1,0:T(8,128)(2,1)S(1)} %copy-done, bf16[128,1,8,1024]{3,2,1,0:T(8,128)(2,1)} %all-to-all-done, bf16[1,1,1024,1024]{3,2,1,0:T(8,128)(2,1)} %param.7), kind=kOutput, calls=%fused_computation.8 | convolution fusion | flops 4298113024 | bytes 10485764 | tf_op jit(solution)/shard_map/dot_general | solution.py:58
  112.3 2.8 %fusion.5 = bf16[1,128,8,1024]{3,2,1,0:T(8,128)(2,1)S(1)} fusion(f32[1024,1024]{0,1:T(8,128)} %get-tuple-element.6, f32[]{:T(128)S(6)} %sqrt.7), kind=kLoop, calls=%fused_computation.10 | loop fusion | flops 2097152 | bytes 6291460 | tf_op jit(solution)/shard_map/reshape | solution.py:61
  116.6 55.4 %all_to_all.14 = bf16[128,1,1,8,1024]{4,3,2,1,0:T(8,128)(2,1)S(1)} all-to-all(bf16[128,1,1,8,1024]{4,3,2,1,0:T(8,128)(2,1)S(1)} %constant_dynamic-update-slice_fusion), channel_id=1, replica_groups=mesh['dp_0'=4,'dp_1'=8,'dp_2'=4,'mp'=2] {'dp_0','dp_1','dp_2'}, dimensions={0} | all-to-all | bytes 4194304 | tf_op jit(solution)/shard_map/all_to_all | solution.py:17
  171.9 1.7 convert_bitcast_fusion
  173.6 3.0 %copy.4074 = bf16[32,8,4,1024]{3,2,1,0:T(4,128)(2,1)} copy(bf16[32,8,4,1024]{3,0,2,1:T(8,128)(2,1)S(1)} %convert_bitcast_fusion) | data formatting | bytes 4194304 | tf_op jit(solution)/shard_map/convert_element_type | solution.py:69
  176.6 4.5 %reshape.32 = bf16[32,8,4096]{2,1,0:T(8,128)(2,1)} reshape(bf16[32,8,4,1024]{3,2,1,0:T(4,128)(2,1)} %copy.4074) | data formatting | bytes 4194304 | tf_op jit(solution)/shard_map/reshape | solution.py:69
  (129 shorter events, 0.5 us)
Async XLA Ops:
  0.0 102.3 %copy-start = (bf16[1,1,1024,1024]{3,2,1,0:T(8,128)(2,1)S(1)}, bf16[1,1,1024,1024]{3,2,1,0:T(8,128)(2,1)}, u32[]{:S(2)}) copy-start(bf16[1,1,1024,1024]{3,2,1,0:T(8,128)(2,1)} %param.8) | copy-start | bytes 6291460
  7.7 15.6 %copy-start.1 = (s32[2,32,4]{1,2,0:T(4,128)S(1)}, s32[2,32,4]{1,2,0:T(4,128)}, u32[]{:S(2)}) copy-start(s32[2,32,4]{1,2,0:T(4,128)} %param.9) | copy-start | bytes 3076
  7.7 94.6 %all-to-all-start = ((bf16[128,1,8,1024]{3,2,1,0:T(8,128)(2,1)}), bf16[128,1,8,1024]{3,2,1,0:T(8,128)(2,1)}, u32[]{:S(2)}, u32[]{:S(2)}) async-start(bf16[128,1,8,1024]{3,2,1,0:T(8,128)(2,1)} %copy.4071), calls=%async_computation | async-start | bytes 4194304 | tf_op jit(solution)/shard_map/all_to_all | solution.py:53

commit v2 on v0

--- a/solution.py
+++ b/solution.py
@@ -12,7 +12,11 @@
 
 def one_axis_at_a_time(value, axes):
     for axis in axes:
-        value = lax.psum(value, axis)
+
+        def leaf_place(local):
+            return jnp.sum(lax.all_gather(local, axis), axis=0)
+
+        value = leaf_place(value)
     return value
 
 

time: 171 us -> 176 us (1.029)
  blocking collectives: 117 us -> 122 us
    all_gather x0 -> x3, blocking collectives: none -> 67.4 us  [leaf_place(): return jnp.sum(lax.all_gather(local, axis), axis=0)]
    psum x3 -> x0, blocking collectives: 58.2 us -> none  [one_axis_at_a_time(): value = lax.psum(value, axis)]
    all_to_all x1, blocking collectives: 58.6 us -> 54.7 us  [per_device(): back = lax.all_to_all(result, DP, split_axis=1, concat_axis=0, tiled=True)]
  transfers between devices with their start and end apart: 1 -> 1, of which waited for: 0 -> 0; matrix products, arithmetic and copies ran while one was open for 5% -> 4% of each run, Pallas kernels for 0% -> 0%
where the time goes in v2:
time: 176 us
  blocking collectives  122 us (69%)
  starting transfers between devices  15.6 us (9%)
  matrix products  15.3 us (9%)
  local copies, waits for them, and re-layouts  11.6 us (7%)
  other arithmetic  9.67 us (5%)
    all_gather x3, blocking collectives, leaf_place(): return jnp.sum(lax.all_gather(local, axis), axis=0)  67.4 us
    all_to_all x1, blocking collectives, per_device(): back = lax.all_to_all(result, DP, split_axis=1, concat_axis=0, tiled=True)  54.7 us
    all_to_all x1, starting transfers between devices, per_device(): lax.all_to_all(outgoing, DP, split_axis=0, concat_axis=1, tiled=True)  15.6 us
    dot_general x1, matrix products, per_device(): shaped = jnp.dot(left, mixed, preferred_element_type=jnp.float32)  9.25 us
    reduce_sum x2, other arithmetic, per_device(): jnp.sum((direction * direction).reshape(row_blocks, block_rows, col_block...  6.16 us
    reshape x1, local copies, waits for them, and re-layouts, per_device(): placed.astype(jnp.bfloat16).reshape(row_blocks, block_rows, half_cols)  4.45 us
    dot_general x1, matrix products, per_device(): jnp.einsum('src,rwck->swk', select_half, tiles, preferred_element_type=jn...  4.35 us
  transfers between devices with their start and end apart: 1, of which 0 were waited for; matrix products, arithmetic and copies ran while one was open for 4% of the time, Pallas kernels for 0%

profile of v2, /device:TPU:32, one launch (start us, length us, event | category | flops | bytes accessed | tf_op | source)
XLA Modules:
  0.0 175.8 jit_solution(18205387848069560403)
XLA Ops:
  0.0 0.0 copy-start
  0.0 0.8 fusion.41
  0.8 4.4 %fusion.18 = bf16[128,1,8,1024]{3,0,2,1:T(8,128)(2,1)S(1)} fusion(bf16[32,8,4,1024]{3,1,2,0:T(8,128)(2,1)} %bitcast.62, s32[32,4]{0,1:T(4,128)S(1)} %fusion.41), kind=kOutput, calls=%fused_computation.22 | convolution fusion | flops 269500416 | bytes 4194816 | tf_op jit(solution)/shard_map/src,rwck->swk/dot_general | solution.py:42
  5.2 2.5 %copy.29 = bf16[128,1,8,1024]{3,2,1,0:T(8,128)(2,1)} copy(bf16[128,1,8,1024]{3,0,2,1:T(8,128)(2,1)S(1)} %fusion.18) | data formatting | bytes 4194304 | tf_op jit(solution)/shard_map/reshape | solution.py:43
  7.7 0.0 copy-start.1
  7.7 15.6 %all-to-all-start = ((bf16[128,1,8,1024]{3,2,1,0:T(8,128)(2,1)}), bf16[128,1,8,1024]{3,2,1,0:T(8,128)(2,1)}, u32[]{:S(2)}, u32[]{:S(2)}) async-start(bf16[128,1,8,1024]{3,2,1,0:T(8,128)(2,1)} %copy.29), calls=%async_computation | async-start | bytes 4194304 | tf_op jit(solution)/shard_map/all_to_all | solution.py:49
  23.3 0.0 copy-done.1
  23.3 0.1 copy.30
  23.4 0.1 eq.28
  23.5 6.0 %fusion.4 = f32[32,4096]{1,0:T(8,128)S(1)} fusion(f32[32,8,4096]{2,1,0:T(8,128)} %param.6, bf16[32,8,4096]{2,1,0:T(8,128)(2,1)} %param.5), kind=kLoop, calls=%fused_computation.9 | loop fusion | flops 9306112 | bytes 6815744 | tf_op jit(solution)/shard_map/reduce_sum | solution.py:33
  29.5 0.4 reduce_sum.62
  29.9 0.1 reduce_sum.63
  30.0 0.1 copy.38
  30.1 11.5 %all-gather.3 = f32[4,32,4]{1,2,0:T(4,128)S(1)} all-gather(f32[1,32,4]{1,2,0:T(4,128)S(1)} %bitcast.63), channel_id=2, replica_groups=mesh['dp_0'=4,'dp_1'=8,'dp_2'=4,'mp'=2] {'dp_0'}, dimensions={0}, use_global_device_ids=true | all-gather | bytes 2560 | tf_op jit(solution)/shard_map/all_gather | solution.py:17
  41.6 44.7 %all-gather.4 = f32[8,32,4]{1,2,0:T(4,128)S(1)} all-gather(f32[1,32,4]{1,2,0:T(4,128)S(1)} %bitcast.65), channel_id=3, replica_groups=mesh['dp_0'=4,'dp_1'=8,'dp_2'=4,'mp'=2] {'dp_1'}, dimensions={0}, use_global_device_ids=true | all-gather | bytes 4608 | tf_op jit(solution)/shard_map/all_gather | solution.py:17
  86.3 11.3 %all-gather.5 = f32[4,32,4]{1,2,0:T(4,128)S(1)} all-gather(f32[1,32,4]{1,2,0:T(4,128)S(1)} %bitcast.64), channel_id=4, replica_groups=mesh['dp_0'=4,'dp_1'=8,'dp_2'=4,'mp'=2] {'dp_2'}, dimensions={0}, use_global_device_ids=true | all-gather | bytes 2560 | tf_op jit(solution)/shard_map/all_gather | solution.py:17
  97.6 0.1 copy.32
  97.6 0.1 reshape.37
  97.8 0.7 fusion.36
  99.1 0.0 all-to-all-done
  99.1 0.0 copy-done
  99.2 9.2 %multiply_reduce_fusion = (f32[]{:T(128)}, f32[1024,1024]{0,1:T(8,128)}) fusion(bf16[1,1,1024,1024]{3,2,1,0:T(8,128)(2,1)S(1)} %copy-done, bf16[128,1,8,1024]{3,2,1,0:T(8,128)(2,1)} %all-to-all-done, bf16[1,1,1024,1024]{3,2,1,0:T(8,128)(2,1)} %param.7), kind=kOutput, calls=%fused_computation.8 | convolution fusion | flops 4298113024 | bytes 10485764 | tf_op jit(solution)/shard_map/dot_general | solution.py:54
  109.1 2.8 %fusion.5 = bf16[1,128,8,1024]{3,2,0,1:T(8,128)(2,1)S(1)} fusion(f32[1024,1024]{0,1:T(8,128)} %get-tuple-element.6, f32[]{:T(128)S(6)} %sqrt.7), kind=kLoop, calls=%fused_computation.10 | loop fusion | flops 2097152 | bytes 6291460 | tf_op jit(solution)/shard_map/reshape | solution.py:57
  111.9 54.7 %all_to_all.8 = bf16[1,128,8,1024]{3,2,0,1:T(8,128)(2,1)S(1)} all-to-all(bf16[1,128,8,1024]{3,2,0,1:T(8,128)(2,1)S(1)} %fusion.5), channel_id=1, replica_groups=mesh['dp_0'=4,'dp_1'=8,'dp_2'=4,'mp'=2] {'dp_0','dp_1','dp_2'}, dimensions={1} | all-to-all | bytes 4194304 | tf_op jit(solution)/shard_map/all_to_all | solution.py:58
  166.7 1.7 convert_bitcast_fusion
  168.4 3.0 %copy.35 = bf16[32,8,4,1024]{3,2,1,0:T(4,128)(2,1)} copy(bf16[32,8,4,1024]{3,0,2,1:T(8,128)(2,1)S(1)} %convert_bitcast_fusion) | data formatting | bytes 4194304 | tf_op jit(solution)/shard_map/convert_element_type | solution.py:65
  171.4 4.5 %reshape.40 = bf16[32,8,4096]{2,1,0:T(8,128)(2,1)} reshape(bf16[32,8,4,1024]{3,2,1,0:T(4,128)(2,1)} %copy.35) | data formatting | bytes 4194304 | tf_op jit(solution)/shard_map/reshape | solution.py:65
  (4 shorter events, 0.1 us)
Async XLA Ops:
  0.0 99.1 %copy-start = (bf16[1,1,1024,1024]{3,2,1,0:T(8,128)(2,1)S(1)}, bf16[1,1,1024,1024]{3,2,1,0:T(8,128)(2,1)}, u32[]{:S(2)}) copy-start(bf16[1,1,1024,1024]{3,2,1,0:T(8,128)(2,1)} %param.8) | copy-start | bytes 6291460
  7.7 15.6 %copy-start.1 = (s32[2,32,4]{1,2,0:T(4,128)S(1)}, s32[2,32,4]{1,2,0:T(4,128)}, u32[]{:S(2)}) copy-start(s32[2,32,4]{1,2,0:T(4,128)} %param.9) | copy-start | bytes 3076
  7.7 91.5 %all-to-all-start = ((bf16[128,1,8,1024]{3,2,1,0:T(8,128)(2,1)}), bf16[128,1,8,1024]{3,2,1,0:T(8,128)(2,1)}, u32[]{:S(2)}, u32[]{:S(2)}) async-start(bf16[128,1,8,1024]{3,2,1,0:T(8,128)(2,1)} %copy.29), calls=%async_computation | async-start | bytes 4194304 | tf_op jit(solution)/shard_map/all_to_all | solution.py:49
